TPU v7x, 32 devices: a whole 2x2x4 slice. The times are simulated.
32 devices in a mesh: win: 2 (over y), row: 16 (over z, x, core).
Axes of the slice: x: 2, y: 2, z: 4, core: 2. Of those that a mesh axis runs over, the one named last changes fastest.
Arguments:
- spectra: bfloat16 [32, 2, 32768], P(('win', 'row')), parts along dimension 0, may hold values from -6 to 6
- pair_mask: int32 [16, 16], P('row'), may hold values from 0 to 1, as said below
- available: int32 [32], P('win'), parts along dimension 0, may hold values 0 or 1
Outputs:
- correlations: float32 [32, 16, 8192], P(('win', 'row')), parts along dimension 0
There are 2 independent parts, one for each index of `win`. A program takes and returns all parts, laid end to end along the dimension named above; an argument that names none is the same for every part. Nothing has to cross between parts.
Inputs may be any that keep to these rules, and one draw needn't show every extreme that they name: pair_mask[i, j] is 0 wherever j <= i.
All inputs are finite; a program needn't handle non-finite values.
Results may differ from a plain program's by a relative error of at most 0.0003.
Values may be sent and summed in bfloat16 or wider, within the bound.
A program may use at most 128 MiB of HBM per device.

v0:
```python
import math
import jax
import jax.numpy as jnp
from jax import lax
from jax.sharding import PartitionSpec as P

LAGS = 8192
full_turn = 2.0 * math.pi


def shifted(value, axis, by):
    size = lax.axis_size(axis)
    return lax.ppermute(value, axis, [(i, (i + by) % size) for i in range(size)])


def build_tables(freq, lags):
    nfft = 2 * freq
    inner = min(128, lags // 2)
    column = nfft // inner
    depth = freq // column
    outer = lags // inner
    centre = lags // 2
    t_inner = jnp.arange(inner, dtype=jnp.int32)
    k_depth = jnp.arange(depth, dtype=jnp.int32)
    k_column = jnp.arange(column, dtype=jnp.int32)
    t_outer = jnp.arange(outer, dtype=jnp.int32)
    first = full_turn * (t_inner[:, None] * k_depth[None, :] % inner).astype(jnp.float32) / inner
    cos_first = jnp.cos(first)
    sin_first = jnp.sin(first)
    section_one = jnp.concatenate(
        [
            jnp.concatenate([cos_first, -sin_first], axis=1),
            jnp.concatenate([sin_first, cos_first], axis=1),
        ],
        axis=0,
    )
    twist = (
        full_turn
        * jnp.mod(k_column[None, :] * (t_inner[:, None] - centre), nfft).astype(jnp.float32)
        / nfft
    )
    second = (
        full_turn * (t_outer[:, None] * k_column[None, :] % column).astype(jnp.float32) / column
    )
    section_two = jnp.stack([jnp.cos(second), -jnp.sin(second)], axis=1)
    return (section_one, jnp.cos(twist), jnp.sin(twist), section_two)


def pair_block(own_wide, part, signs, tables):
    section_one, twist_cos, twist_sin, section_two = tables
    count = own_wide.shape[0]
    width = part.shape[0]
    freq = part.shape[2]
    inner = twist_cos.shape[0]
    column = twist_cos.shape[1]
    outer = section_two.shape[0]
    depth = freq // column
    other = part.astype(jnp.float32)
    real_part = (
        own_wide[:, None, 0, :] * other[None, :, 0, :]
        + own_wide[:, None, 1, :] * other[None, :, 1, :]
    )
    imag_part = (
        own_wide[:, None, 0, :] * other[None, :, 1, :]
        - own_wide[:, None, 1, :] * other[None, :, 0, :]
    ) * signs[:, :, None]
    cross = jnp.stack([real_part, imag_part], axis=2).reshape(count * width, 2 * depth, column)
    mixed = jnp.einsum("uv,pvk->puk", section_one, cross, precision=lax.Precision.HIGH)
    mixed = mixed.reshape(count * width, 2, inner, column)
    turned_real = mixed[:, 0] * twist_cos - mixed[:, 1] * twist_sin
    turned_imag = mixed[:, 0] * twist_sin + mixed[:, 1] * twist_cos
    turned = jnp.stack([turned_real, turned_imag], axis=1)
    summed = jnp.einsum("tck,pcuk->ptu", section_two, turned, precision=lax.Precision.HIGH)
    summed = summed.reshape(count, width, outer * inner)
    return (2.0 * summed - real_part[:, :, :1]) * (1.0 / math.sqrt(8.0 * freq))


def correlate(own, others, signs, tables):
    own_wide = own.astype(jnp.float32)
    count = own.shape[0]
    total = others.shape[0]
    width = math.gcd(total, max(1, 8 // count))
    if width == total:
        return pair_block(own_wide, others, signs, tables)
    groups = total // width
    pieces = others.reshape(groups, width, 2, others.shape[2])
    sign_pieces = jnp.transpose(signs.reshape(count, groups, width), (1, 0, 2))

    def one_group(item):
        return pair_block(own_wide, item[0], item[1], tables)

    results = lax.map(one_group, (pieces, sign_pieces))
    return jnp.transpose(results, (1, 0, 2, 3)).reshape(count, total, results.shape[3])


def per_device(spectra, pair_mask, available):
    count = spectra.shape[0]
    devices = lax.axis_size("row")
    stations = count * devices
    freq = spectra.shape[2]
    tables = build_tables(freq, LAGS)
    first_station = lax.axis_index("row") * count
    own_flags = lax.dynamic_slice_in_dim(available, first_station, count, 0).astype(jnp.float32)
    weight = (
        pair_mask.astype(jnp.float32) * own_flags[:, None] * available.astype(jnp.float32)[None, :]
    )
    reach = devices // 2 + 1
    window = spectra
    have = 1
    while have < reach:
        take = min(have, reach - have)
        moved = shifted(window[: take * count], "row", -have)
        window = jnp.concatenate([window, moved], axis=0)
        have = have + take
    half = stations // 2
    offsets = jnp.arange(half, dtype=jnp.int32) + 1
    columns = jnp.arange(stations, dtype=jnp.int32)
    station = first_station + 0
    signs = jnp.where(station + offsets >= stations, -1.0, 1.0).astype(jnp.float32)[None, :]
    near = correlate(window[0:1], window[1 : 1 + half], signs, tables)[0]
    padded = jnp.concatenate([near, jnp.zeros_like(near)], axis=0)
    placed = jnp.roll(padded, station + 1, axis=0)
    keep_rows = [jnp.where((columns > station)[:, None], placed, 0.0)]
    send_rows = [jnp.where((columns < station - half)[:, None], placed, 0.0)]
    kept = jnp.stack(keep_rows, axis=0)
    outgoing = jnp.stack(send_rows, axis=1)
    incoming = lax.all_to_all(outgoing, "row", split_axis=0, concat_axis=1, tiled=True)
    corr = kept + incoming
    return corr * weight[:, :, None]


def solution(mesh):
    return jax.shard_map(
        per_device,
        mesh=mesh,
        in_specs=(P(("win", "row"), None, None), P("row", None), P("win")),
        out_specs=P(("win", "row"), None, None),
        check_vma=False,
    )
```

profile of v0, /device:TPU:0, one launch (start us, length us, event | category | flops | bytes accessed | tf_op | source)
XLA Modules:
  0.0 77.3 jit_solution(7756633121859793812)
XLA Ops:
  0.0 5.4 %collective-permute-start = (bf16[1,2,32768]{2,1,0:T(2,128)(2,1)}, bf16[1,2,32768]{2,1,0:T(2,128)(2,1)S(1)}, u32[]{:S(2)}, u32[]{:S(2)}) collective-permute-start(bf16[1,2,32768]{2,1,0:T(2,128)(2,1)} %param.3), channel_id=1, source_target_pairs={{0,15},{1,0},{2,1},{3,2},{4,3},{5,4},{6,5},{7,6},{8,7},{9,8},{10,9... | collective-permute-start | bytes 393224 | tf_op jit(solution)/shard_map/ppermute | solution.py:13
  5.4 1.2 %fusion.60 = (f32[1,1,32768]{2,1,0:T(1,128)S(1)}, f32[1,1,32768]{2,1,0:T(1,128)S(1)}) fusion(bf16[1,2,32768]{2,1,0:T(2,128)(2,1)} %param.3), kind=kLoop, calls=%fused_computation.92 | loop fusion | bytes 524288 | tf_op jit(solution)/shard_map/slice | solution.py:60
  6.7 1.6 %collective-permute-done = bf16[1,2,32768]{2,1,0:T(2,128)(2,1)S(1)} collective-permute-done((bf16[1,2,32768]{2,1,0:T(2,128)(2,1)}, bf16[1,2,32768]{2,1,0:T(2,128)(2,1)S(1)}, u32[]{:S(2)}, u32[]{:S(2)}) %collective-permute-start) | collective-permute-done | bytes 131104 | tf_op jit(solution)/shard_map/ppermute | solution.py:13
  8.3 1.3 %pad_maximum_fusion.2 = bf16[2,2,32768]{2,1,0:T(2,128)(2,1)S(1)} fusion(bf16[1,2,32768]{2,1,0:T(2,128)(2,1)S(1)} %collective-permute-done, bf16[1,2,32768]{2,1,0:T(2,128)(2,1)} %param.3), kind=kLoop, calls=%fused_computation.37 | loop fusion | flops 131072 | bytes 524288 | tf_op jit(solution)/shard_map/concatenate | solution.py:113
  9.6 0.6 collective-permute-start.1
  10.2 0.9 %fusion.54 = f32[128,64]{1,0:T(8,128)} fusion(), kind=kLoop, calls=%fused_computation.79 | loop fusion | flops 122880 | bytes 32768 | tf_op jit(solution)/shard_map/neg | solution.py:32
  11.1 0.9 %fusion.52 = (f32[128,64]{1,0:T(8,128)}, f32[128,64]{1,0:T(8,128)}) fusion(), kind=kLoop, calls=%fused_computation.77 | loop fusion | flops 114688 | bytes 65536 | tf_op jit(solution)/shard_map/sin | solution.py:29
  12.0 5.5 %collective-permute-done.1 = bf16[2,2,32768]{2,1,0:T(2,128)(2,1)S(1)} collective-permute-done((bf16[2,2,32768]{2,1,0:T(2,128)(2,1)S(1)}, bf16[2,2,32768]{2,1,0:T(2,128)(2,1)S(1)}, u32[]{:S(2)}, u32[]{:S(2)}) %collective-permute-start.1) | collective-permute-done | bytes 262176 | tf_op jit(solution)/shard_map/ppermute | solution.py:13
  17.5 1.7 %pad_maximum_fusion.1 = bf16[4,2,32768]{2,1,0:T(2,128)(2,1)S(1)} fusion(bf16[2,2,32768]{2,1,0:T(2,128)(2,1)S(1)} %collective-permute-done.1, bf16[1,2,32768]{2,1,0:T(2,128)(2,1)S(1)} %collective-permute-done, bf16[1,2,32768]{2,1,0:T(2,128)(2,1)} %param.3), kind=kLoop, calls=%fused_computation.25 | loop fusion | flops 524288 | bytes 1048576 | tf_op jit(solution)/shard_map/concatenate | solution.py:113
  19.2 0.4 collective-permute-start.2
  19.6 1.9 %fusion.43 = (f32[128,512]{1,0:T(8,128)S(1)}, f32[128,512]{1,0:T(8,128)}) fusion(s32[128]{0:T(128)S(1)} %iota_add_fusion), kind=kLoop, calls=%fused_computation.63 | loop fusion | flops 917504 | bytes 524800 | tf_op jit(solution)/shard_map/cos | solution.py:46
  21.5 0.6 slice.42
  22.0 0.5 slice.44
  22.6 1.2 %sine_negate_fusion = (f32[64,1,512]{2,0,1:T(8,128)S(1)}, f32[64,1,512]{2,0,1:T(8,128)}) fusion(), kind=kLoop, calls=%fused_computation.59 | loop fusion | flops 491520 | bytes 262144 | tf_op jit(solution)/shard_map/neg | solution.py:45
  23.8 9.3 %collective-permute-done.2 = bf16[4,2,32768]{2,1,0:T(2,128)(2,1)S(1)} collective-permute-done((bf16[4,2,32768]{2,1,0:T(2,128)(2,1)S(1)}, bf16[4,2,32768]{2,1,0:T(2,128)(2,1)S(1)}, u32[]{:S(2)}, u32[]{:S(2)}) %collective-permute-start.2) | collective-permute-done | bytes 524320 | tf_op jit(solution)/shard_map/ppermute | solution.py:13
  33.1 1.4 %maximum_convert_fusion = f32[8,2,32768]{2,1,0:T(2,128)S(1)} fusion(bf16[1,2,32768]{2,1,0:T(2,128)(2,1)S(1)} %collective-permute-done.3, bf16[4,2,32768]{2,1,0:T(2,128)(2,1)S(1)} %collective-permute-done.2, bf16[2,2,32768]{2,1,0:T(2,128)(2,1)S(1)} %collective-permute-done.1, bf16[1,2,32768]{2,1,0:T(2,128)(2,1)S(1)} %collective-permute-done), kind=kLoop, calls=%fused_computation.10 | loop fusion | flops 2097152 | bytes 3145728 | tf_op jit(solution)/shard_map/convert_element_type | solution.py:58
  34.5 3.0 %slice_bitcast_fusion.1 = (f32[1,8,32768]{2,0,1:T(1,128)S(1)}, f32[1,8,32768]{2,0,1:T(1,128)}) fusion(f32[8,2,32768]{2,1,0:T(2,128)S(1)} %maximum_convert_fusion), kind=kLoop, calls=%fused_computation.76 | loop fusion | bytes 4194304 | tf_op jit(solution)/shard_map/broadcast_in_dim;squeeze | solution.py:60
  37.5 2.6 %fusion.13 = (f32[1,8,1,32768]{3,2,1,0:T(1,128)S(1)}, f32[1,8,1,32768]{3,2,1,0:T(1,128)S(1)}) fusion(f32[32768]{0:T(1024)S(1)} %bitcast.65, f32[32768]{0:T(1024)S(1)} %bitcast.63, f32[8,2,32768]{2,1,0:T(2,128)S(1)} %maximum_convert_fusion, f32[8]{0:T(128)S(1)} %compare_select_fusion), kind=kLoop, calls=%fused_computation.17 | loop fusion | flops 1835008 | bytes 4456480 | tf_op jit(solution)/shard_map/add | solution.py:60
  40.1 3.2 %pad_maximum_fusion = f32[1,8,2,32768]{3,2,1,0:T(2,128)} fusion(f32[1,8,1,32768]{3,2,1,0:T(1,128)S(1)} %get-tuple-element.8, f32[1,8,1,32768]{3,2,1,0:T(1,128)S(1)} %get-tuple-element.7), kind=kLoop, calls=%fused_computation.4 | loop fusion | flops 524288 | bytes 4194304 | tf_op jit(solution)/shard_map/stack | solution.py:67
  43.3 3.2 %reshape.460 = f32[8,128,512]{2,1,0:T(8,128)S(1)} reshape(f32[1,8,2,32768]{3,2,1,0:T(2,128)} %pad_maximum_fusion) | data formatting | bytes 4194304 | tf_op jit(solution)/shard_map/reshape | solution.py:67
  46.5 0.0 copy-start
  46.6 3.2 %fusion.33 = f32[8,512,256]{1,2,0:T(8,128)S(1)} fusion(f32[8,128,512]{2,1,0:T(8,128)S(1)} %reshape.460, f32[128,64]{1,0:T(8,128)} %get-tuple-element.16, f32[128,64]{1,0:T(8,128)} %get-tuple-element.15, f32[128,64]{1,0:T(8,128)} %fusion.54), kind=kOutput, calls=%fused_computation.52 | convolution fusion | flops 805404672 | bytes 6389760 | tf_op jit(solution)/shard_map/uv,pvk->puk/dot_general | solution.py:68
  49.8 0.7 multiply_subtract_fusion
  50.5 2.1 %fusion.56 = f32[8]{0:T(128)S(1)} fusion(f32[1,8,32768]{2,0,1:T(1,128)} %get-tuple-element.10, f32[1,8,32768]{2,0,1:T(1,128)S(1)} %get-tuple-element.9, f32[1]{0:T(128)} %slice.44, f32[1]{0:T(128)} %slice.42), kind=kLoop, calls=%fused_computation.83 | loop fusion | flops 24 | bytes 104 | tf_op jit(solution)/shard_map/slice | solution.py:75
  52.5 2.0 %fusion.10 = f32[1,8,64,128]{3,2,1,0:T(8,128)S(1)} fusion(f32[8,1,128,512]{3,2,1,0:T(8,128)S(1)} %get-tuple-element.6, f32[8,1,128,512]{3,2,1,0:T(8,128)S(1)} %get-tuple-element.5, f32[64,1,512]{2,0,1:T(8,128)S(1)} %get-tuple-element.17, f32[64,1,512]{2,0,1:T(8,128)S(1)} %copy-done.1), kind=kOutput, calls=%fused_computation.9 | convolution fusion | flops 403832832 | bytes 4718592 | tf_op jit(solution)/shard_map/tck,pcuk->ptu/dot_general | solution.py:73
  54.6 0.2 fusion.24
  54.8 0.3 broadcast_select_fusion
  55.1 1.3 %stack.22 = f32[16,1,8192]{2,1,0:T(1,128)} reshape(f32[16,8192]{1,0:T(8,128)S(1)} %broadcast_select_fusion) | data formatting | bytes 1048576 | tf_op jit(solution)/shard_map/stack | solution.py:126
  56.4 5.4 %all-to-all-start = ((f32[16,1,8192]{2,1,0:T(1,128)}), f32[16,1,8192]{2,1,0:T(1,128)S(1)}, u32[]{:S(2)}, u32[]{:S(2)}) async-start(f32[16,1,8192]{2,1,0:T(1,128)} %stack.22), calls=%async_computation | async-start | bytes 1048576 | tf_op jit(solution)/shard_map/all_to_all | solution.py:127
  61.8 0.6 dynamic_slice.8
  63.1 13.0 %all-to-all-done = f32[16,1,8192]{2,1,0:T(1,128)S(1)} async-done(((f32[16,1,8192]{2,1,0:T(1,128)}), f32[16,1,8192]{2,1,0:T(1,128)S(1)}, u32[]{:S(2)}, u32[]{:S(2)}) %all-to-all-start) | async-done | bytes 524320 | tf_op jit(solution)/shard_map/all_to_all | solution.py:127
  76.1 1.2 %fusion.20 = f32[1,16,8192]{2,1,0:T(8,128)} fusion(f32[16,1,8192]{2,1,0:T(1,128)S(1)} %all-to-all-done, f32[16]{0:T(128)S(1)} %fusion.57, pred[16]{0:T(512)(128)(4,1)S(1)} %iota_compare_fusion.1, s32[]{:T(128)S(6)} %select_n.86, f32[8,8192]{1,0:T(8,128)S(1)} %broadcast_in_dim.49, f32[8,8192]{1,0:T(8,128)S(1)} %fusion.24), kind=kLoop, calls=%fused_computation.28 | loop fusion | flops 786432 | bytes 1572948 | tf_op jit(solution)/shard_map/mul | solution.py:129
  (15 shorter events, 0.1 us)
Async XLA Ops:
  0.0 8.3 %collective-permute-start = (bf16[1,2,32768]{2,1,0:T(2,128)(2,1)}, bf16[1,2,32768]{2,1,0:T(2,128)(2,1)S(1)}, u32[]{:S(2)}, u32[]{:S(2)}) collective-permute-start(bf16[1,2,32768]{2,1,0:T(2,128)(2,1)} %param.3), channel_id=1, source_target_pairs={{0,15},{1,0},{2,1},{3,2},{4,3},{5,4},{6,5},{7,6},{8,7},{9,8},{10,9... | collective-permute-start | bytes 393224 | tf_op jit(solution)/shard_map/ppermute | solution.py:13
  5.4 18.3 %collective-permute-start.3 = (bf16[1,2,32768]{2,1,0:T(2,128)(2,1)}, bf16[1,2,32768]{2,1,0:T(2,128)(2,1)S(1)}, u32[]{:S(2)}, u32[]{:S(2)}) collective-permute-start(bf16[1,2,32768]{2,1,0:T(2,128)(2,1)} %param.3), channel_id=1, source_target_pairs={{0,8},{1,9},{2,10},{3,11},{4,12},{5,13},{6,14},{7,15},{8,0},{9,1},... | collective-permute-start | bytes 393224 | tf_op jit(solution)/shard_map/ppermute | solution.py:13
  9.6 8.0 %collective-permute-start.1 = (bf16[2,2,32768]{2,1,0:T(2,128)(2,1)S(1)}, bf16[2,2,32768]{2,1,0:T(2,128)(2,1)S(1)}, u32[]{:S(2)}, u32[]{:S(2)}) collective-permute-start(bf16[2,2,32768]{2,1,0:T(2,128)(2,1)S(1)} %pad_maximum_fusion.2), channel_id=1, source_target_pairs={{0,14},{1,15},{2,0},{3,1},{4,2},{5,3},{6,4},{7,5},{8,6},{9,7},{10,... | collective-permute-start | bytes 786440 | tf_op jit(solution)/shard_map/ppermute | solution.py:13
  19.2 13.9 %collective-permute-start.2 = (bf16[4,2,32768]{2,1,0:T(2,128)(2,1)S(1)}, bf16[4,2,32768]{2,1,0:T(2,128)(2,1)S(1)}, u32[]{:S(2)}, u32[]{:S(2)}) collective-permute-start(bf16[4,2,32768]{2,1,0:T(2,128)(2,1)S(1)} %pad_maximum_fusion.1), channel_id=1, source_target_pairs={{0,12},{1,13},{2,14},{3,15},{4,0},{5,1},{6,2},{7,3},{8,4},{9,5},{1... | collective-permute-start | bytes 1572872 | tf_op jit(solution)/shard_map/ppermute | solution.py:13
  46.5 3.2 %copy-start = (f32[128,512]{1,0:T(8,128)S(1)}, f32[128,512]{1,0:T(8,128)}, u32[]{:S(2)}) copy-start(f32[128,512]{1,0:T(8,128)} %get-tuple-element.14) | copy-start | bytes 786436
  49.8 2.8 %copy-start.1 = (f32[64,1,512]{2,0,1:T(8,128)S(1)}, f32[64,1,512]{2,0,1:T(8,128)}, u32[]{:S(2)}) copy-start(f32[64,1,512]{2,0,1:T(8,128)} %get-tuple-element.18) | copy-start | bytes 393220
  54.6 7.3 %copy-start.2 = (s32[16]{0:T(128)S(1)}, s32[16]{0:T(128)}, u32[]{:S(2)}) copy-start(s32[16]{0:T(128)} %param.5) | copy-start | bytes 196
  54.6 8.5 %copy-start.3 = (s32[1,16]{1,0:T(1,128)S(1)}, s32[1,16]{1,0:T(1,128)}, u32[]{:S(2)}) copy-start(s32[1,16]{1,0:T(1,128)} %param.4) | copy-start | bytes 196
  56.4 19.7 %all-to-all-start = ((f32[16,1,8192]{2,1,0:T(1,128)}), f32[16,1,8192]{2,1,0:T(1,128)S(1)}, u32[]{:S(2)}, u32[]{:S(2)}) async-start(f32[16,1,8192]{2,1,0:T(1,128)} %stack.22), calls=%async_computation | async-start | bytes 1048576 | tf_op jit(solution)/shard_map/all_to_all | solution.py:127
where the time goes:
time: 77.7 us; the launch traced here: 77.3 us
  waiting for transfers between devices  29.4 us (38%)
  other arithmetic  19.5 us (25%)
  starting transfers between devices  11.9 us (15%)
  local copies, waits for them, and re-layouts  10.5 us (14%)
  matrix products  5.22 us (7%)
  between operations  0.79 us (1%)
    ppermute x4, waiting for transfers between devices, shifted(): lax.ppermute(value, axis, [(i, (i + by) % size) for i in range(size)])  16.4 us
    all_to_all x1, waiting for transfers between devices, per_device(): lax.all_to_all(outgoing, 'row', split_axis=0, concat_axis=1, tiled=True)  13 us
    ppermute x4, starting transfers between devices, shifted(): lax.ppermute(value, axis, [(i, (i + by) % size) for i in range(size)])  6.45 us
    all_to_all x1, starting transfers between devices, per_device(): lax.all_to_all(outgoing, 'row', split_axis=0, concat_axis=1, tiled=True)  5.41 us
    reshape x1, local copies, waits for them, and re-layouts, pair_block(): jnp.stack([real_part, imag_part], axis=2)  3.23 us
    another operation x1, other arithmetic, pair_block(): jnp.stack([real_part, imag_part], axis=2)  3.2 us
    dot_general x1, matrix products, pair_block(): jnp.einsum('uv,pvk->puk', section_one, cross, precision=lax.Precision.HIGH)  3.19 us
    another operation x1, local copies, waits for them, and re-layouts, pair_block(): other[None, :, 0, :]  2.99 us
  transfers between devices with their start and end apart: 5, of which 4 were waited for; matrix products, arithmetic and copies ran while one was open for 14% of the time, Pallas kernels for 0%

commit v1 on v0

--- a/solution.py
+++ b/solution.py
@@ -124,7 +124,10 @@
     send_rows = [jnp.where((columns < station - half)[:, None], placed, 0.0)]
     kept = jnp.stack(keep_rows, axis=0)
     outgoing = jnp.stack(send_rows, axis=1)
-    incoming = lax.all_to_all(outgoing, "row", split_axis=0, concat_axis=1, tiled=True)
+    n_dev = lax.axis_size("row")
+    blocks = jnp.stack(jnp.split(outgoing, n_dev, axis=0), axis=0)
+    blocks = lax.all_to_all(blocks, "row", split_axis=0, concat_axis=0)
+    incoming = jnp.concatenate(blocks, axis=1)
     corr = kept + incoming
     return corr * weight[:, :, None]
 

time: 77.7 us -> 86.7 us (1.12)
  local copies, waits for them, and re-layouts: 10.5 us -> 19.5 us
    unnamed x8 -> x23, local copies, waits for them, and re-layouts: 0.02 us -> 9.65 us
  transfers between devices with their start and end apart: 5 -> 5, of which waited for: 4 -> 4; matrix products, arithmetic and copies ran while one was open for 14% -> 13% of each run, Pallas kernels for 0% -> 0%
where the time goes in v1:
time: 86.7 us; the launch traced here: 86.3 us
  waiting for transfers between devices  29.4 us (34%)
  local copies, waits for them, and re-layouts  19.5 us (22%)
  other arithmetic  19.5 us (22%)
  starting transfers between devices  11.9 us (14%)
  matrix products  5.22 us (6%)
    ppermute x4, waiting for transfers between devices, shifted(): lax.ppermute(value, axis, [(i, (i + by) % size) for i in range(size)])  16.4 us
    all_to_all x1, waiting for transfers between devices, per_device(): blocks = lax.all_to_all(blocks, 'row', split_axis=0, concat_axis=0)  13 us
    unnamed x23, local copies, waits for them, and re-layouts  9.65 us
    ppermute x4, starting transfers between devices, shifted(): lax.ppermute(value, axis, [(i, (i + by) % size) for i in range(size)])  6.45 us
    all_to_all x1, starting transfers between devices, per_device(): blocks = lax.all_to_all(blocks, 'row', split_axis=0, concat_axis=0)  5.41 us
    reshape x1, local copies, waits for them, and re-layouts, pair_block(): jnp.stack([real_part, imag_part], axis=2)  3.23 us
    another operation x1, other arithmetic, pair_block(): jnp.stack([real_part, imag_part], axis=2)  3.2 us
    dot_general x1, matrix products, pair_block(): jnp.einsum('uv,pvk->puk', section_one, cross, precision=lax.Precision.HIGH)  3.19 us
  transfers between devices with their start and end apart: 5, of which 4 were waited for; matrix products, arithmetic and copies ran while one was open for 13% of the time, Pallas kernels for 0%

profile of v1, /device:TPU:0, one launch (start us, length us, event | category | flops | bytes accessed | tf_op | source)
XLA Modules:
  0.0 86.3 jit_solution(9119382263005383643)
XLA Ops:
  0.0 5.4 %collective-permute-start = (bf16[1,2,32768]{2,1,0:T(2,128)(2,1)}, bf16[1,2,32768]{2,1,0:T(2,128)(2,1)S(1)}, u32[]{:S(2)}, u32[]{:S(2)}) collective-permute-start(bf16[1,2,32768]{2,1,0:T(2,128)(2,1)} %param.3), channel_id=1, source_target_pairs={{0,15},{1,0},{2,1},{3,2},{4,3},{5,4},{6,5},{7,6},{8,7},{9,8},{10,9... | collective-permute-start | bytes 393224 | tf_op jit(solution)/shard_map/ppermute | solution.py:13
  5.4 1.2 %fusion.60 = (f32[1,1,32768]{2,1,0:T(1,128)S(1)}, f32[1,1,32768]{2,1,0:T(1,128)S(1)}) fusion(bf16[1,2,32768]{2,1,0:T(2,128)(2,1)} %param.3), kind=kLoop, calls=%fused_computation.124 | loop fusion | bytes 524288 | tf_op jit(solution)/shard_map/slice | solution.py:60
  6.7 1.6 %collective-permute-done = bf16[1,2,32768]{2,1,0:T(2,128)(2,1)S(1)} collective-permute-done((bf16[1,2,32768]{2,1,0:T(2,128)(2,1)}, bf16[1,2,32768]{2,1,0:T(2,128)(2,1)S(1)}, u32[]{:S(2)}, u32[]{:S(2)}) %collective-permute-start) | collective-permute-done | bytes 131104 | tf_op jit(solution)/shard_map/ppermute | solution.py:13
  8.3 1.3 %pad_maximum_fusion.2 = bf16[2,2,32768]{2,1,0:T(2,128)(2,1)S(1)} fusion(bf16[1,2,32768]{2,1,0:T(2,128)(2,1)S(1)} %collective-permute-done, bf16[1,2,32768]{2,1,0:T(2,128)(2,1)} %param.3), kind=kLoop, calls=%fused_computation.37 | loop fusion | flops 131072 | bytes 524288 | tf_op jit(solution)/shard_map/concatenate | solution.py:113
  10.2 0.9 %fusion.54 = f32[128,64]{1,0:T(8,128)} fusion(), kind=kLoop, calls=%fused_computation.111 | loop fusion | flops 122880 | bytes 32768 | tf_op jit(solution)/shard_map/neg | solution.py:32
  11.1 0.9 %fusion.52 = (f32[128,64]{1,0:T(8,128)}, f32[128,64]{1,0:T(8,128)}) fusion(), kind=kLoop, calls=%fused_computation.109 | loop fusion | flops 114688 | bytes 65536 | tf_op jit(solution)/shard_map/sin | solution.py:29
  12.0 5.5 %collective-permute-done.1 = bf16[2,2,32768]{2,1,0:T(2,128)(2,1)S(1)} collective-permute-done((bf16[2,2,32768]{2,1,0:T(2,128)(2,1)S(1)}, bf16[2,2,32768]{2,1,0:T(2,128)(2,1)S(1)}, u32[]{:S(2)}, u32[]{:S(2)}) %collective-permute-start.1) | collective-permute-done | bytes 262176 | tf_op jit(solution)/shard_map/ppermute | solution.py:13
  17.5 1.7 %pad_maximum_fusion.1 = bf16[4,2,32768]{2,1,0:T(2,128)(2,1)S(1)} fusion(bf16[2,2,32768]{2,1,0:T(2,128)(2,1)S(1)} %collective-permute-done.1, bf16[1,2,32768]{2,1,0:T(2,128)(2,1)S(1)} %collective-permute-done, bf16[1,2,32768]{2,1,0:T(2,128)(2,1)} %param.3), kind=kLoop, calls=%fused_computation.25 | loop fusion | flops 524288 | bytes 1048576 | tf_op jit(solution)/shard_map/concatenate | solution.py:113
  19.6 1.9 %fusion.43 = (f32[128,512]{1,0:T(8,128)S(1)}, f32[128,512]{1,0:T(8,128)}) fusion(s32[128]{0:T(128)S(1)} %iota_add_fusion), kind=kLoop, calls=%fused_computation.63 | loop fusion | flops 917504 | bytes 524800 | tf_op jit(solution)/shard_map/cos | solution.py:46
  22.6 1.2 %sine_negate_fusion = (f32[64,1,512]{2,0,1:T(8,128)S(1)}, f32[64,1,512]{2,0,1:T(8,128)}) fusion(), kind=kLoop, calls=%fused_computation.59 | loop fusion | flops 491520 | bytes 262144 | tf_op jit(solution)/shard_map/neg | solution.py:45
  23.8 9.3 %collective-permute-done.2 = bf16[4,2,32768]{2,1,0:T(2,128)(2,1)S(1)} collective-permute-done((bf16[4,2,32768]{2,1,0:T(2,128)(2,1)S(1)}, bf16[4,2,32768]{2,1,0:T(2,128)(2,1)S(1)}, u32[]{:S(2)}, u32[]{:S(2)}) %collective-permute-start.2) | collective-permute-done | bytes 524320 | tf_op jit(solution)/shard_map/ppermute | solution.py:13
  33.1 1.4 %maximum_convert_fusion = f32[8,2,32768]{2,1,0:T(2,128)S(1)} fusion(bf16[1,2,32768]{2,1,0:T(2,128)(2,1)S(1)} %collective-permute-done.3, bf16[4,2,32768]{2,1,0:T(2,128)(2,1)S(1)} %collective-permute-done.2, bf16[2,2,32768]{2,1,0:T(2,128)(2,1)S(1)} %collective-permute-done.1, bf16[1,2,32768]{2,1,0:T(2,128)(2,1)S(1)} %collective-permute-done), kind=kLoop, calls=%fused_computation.10 | loop fusion | flops 2097152 | bytes 3145728 | tf_op jit(solution)/shard_map/convert_element_type | solution.py:58
  34.5 3.0 %slice_bitcast_fusion.1 = (f32[1,8,32768]{2,0,1:T(1,128)S(1)}, f32[1,8,32768]{2,0,1:T(1,128)}) fusion(f32[8,2,32768]{2,1,0:T(2,128)S(1)} %maximum_convert_fusion), kind=kLoop, calls=%fused_computation.76 | loop fusion | bytes 4194304 | tf_op jit(solution)/shard_map/broadcast_in_dim;squeeze | solution.py:60
  37.5 2.6 %fusion.13 = (f32[1,8,1,32768]{3,2,1,0:T(1,128)S(1)}, f32[1,8,1,32768]{3,2,1,0:T(1,128)S(1)}) fusion(f32[32768]{0:T(1024)S(1)} %bitcast.129, f32[32768]{0:T(1024)S(1)} %bitcast.127, f32[8,2,32768]{2,1,0:T(2,128)S(1)} %maximum_convert_fusion, f32[8]{0:T(128)S(1)} %compare_select_fusion), kind=kLoop, calls=%fused_computation.17 | loop fusion | flops 1835008 | bytes 4456480 | tf_op jit(solution)/shard_map/add | solution.py:60
  40.1 3.2 %pad_maximum_fusion = f32[1,8,2,32768]{3,2,1,0:T(2,128)} fusion(f32[1,8,1,32768]{3,2,1,0:T(1,128)S(1)} %get-tuple-element.8, f32[1,8,1,32768]{3,2,1,0:T(1,128)S(1)} %get-tuple-element.7), kind=kLoop, calls=%fused_computation.4 | loop fusion | flops 524288 | bytes 4194304 | tf_op jit(solution)/shard_map/stack | solution.py:67
  43.3 3.2 %reshape.492 = f32[8,128,512]{2,1,0:T(8,128)S(1)} reshape(f32[1,8,2,32768]{3,2,1,0:T(2,128)} %pad_maximum_fusion) | data formatting | bytes 4194304 | tf_op jit(solution)/shard_map/reshape | solution.py:67
  46.6 3.2 %fusion.33 = f32[8,512,256]{1,2,0:T(8,128)S(1)} fusion(f32[8,128,512]{2,1,0:T(8,128)S(1)} %reshape.492, f32[128,64]{1,0:T(8,128)} %get-tuple-element.16, f32[128,64]{1,0:T(8,128)} %get-tuple-element.15, f32[128,64]{1,0:T(8,128)} %fusion.54), kind=kOutput, calls=%fused_computation.52 | convolution fusion | flops 805404672 | bytes 6389760 | tf_op jit(solution)/shard_map/uv,pvk->puk/dot_general | solution.py:68
  49.8 0.7 multiply_subtract_fusion
  50.5 2.1 %fusion.56 = f32[8]{0:T(128)S(1)} fusion(f32[1,8,32768]{2,0,1:T(1,128)} %get-tuple-element.10, f32[1,8,32768]{2,0,1:T(1,128)S(1)} %get-tuple-element.9, f32[1]{0:T(128)} %slice.60, f32[1]{0:T(128)} %slice.58), kind=kLoop, calls=%fused_computation.115 | loop fusion | flops 24 | bytes 104 | tf_op jit(solution)/shard_map/slice | solution.py:75
  52.5 2.0 %fusion.10 = f32[1,8,64,128]{3,2,1,0:T(8,128)S(1)} fusion(f32[8,1,128,512]{3,2,1,0:T(8,128)S(1)} %get-tuple-element.6, f32[8,1,128,512]{3,2,1,0:T(8,128)S(1)} %get-tuple-element.5, f32[64,1,512]{2,0,1:T(8,128)S(1)} %get-tuple-element.17, f32[64,1,512]{2,0,1:T(8,128)S(1)} %copy-done.1), kind=kOutput, calls=%fused_computation.9 | convolution fusion | flops 403832832 | bytes 4718592 | tf_op jit(solution)/shard_map/tck,pcuk->ptu/dot_general | solution.py:73
  55.7 0.6 constant_dynamic-update-slice_fusion.14
  56.3 0.6 constant_dynamic-update-slice_fusion.13
  57.0 0.6 constant_dynamic-update-slice_fusion.12
  57.6 0.6 constant_dynamic-update-slice_fusion.11
  58.3 0.6 constant_dynamic-update-slice_fusion.10
  58.9 0.6 constant_dynamic-update-slice_fusion.9
  59.6 0.6 constant_dynamic-update-slice_fusion.8
  60.8 0.6 constant_dynamic-update-slice_fusion.6
  61.5 0.6 constant_dynamic-update-slice_fusion.5
  65.3 5.4 %all-to-all-start = ((f32[16,1,1,8192]{3,2,1,0:T(1,128)}), f32[16,1,1,8192]{3,2,1,0:T(1,128)S(1)}, u32[]{:S(2)}, u32[]{:S(2)}) async-start(f32[16,1,1,8192]{3,2,1,0:T(1,128)} %constant_dynamic-update-slice_fusion), calls=%async_computation | async-start | bytes 1048576 | tf_op jit(solution)/shard_map/all_to_all | solution.py:129
  72.1 13.0 %all-to-all-done = f32[16,1,1,8192]{3,2,1,0:T(1,128)S(1)} async-done(((f32[16,1,1,8192]{3,2,1,0:T(1,128)}), f32[16,1,1,8192]{3,2,1,0:T(1,128)S(1)}, u32[]{:S(2)}, u32[]{:S(2)}) %all-to-all-start) | async-done | bytes 524320 | tf_op jit(solution)/shard_map/all_to_all | solution.py:129
  85.0 1.2 %fusion.20 = f32[1,16,8192]{2,1,0:T(8,128)} fusion(f32[16,1,1,8192]{3,2,1,0:T(1,128)S(1)} %all-to-all-done, f32[16]{0:T(128)S(1)} %fusion.57, pred[16]{0:T(512)(128)(4,1)S(1)} %iota_compare_fusion.1, s32[]{:T(128)S(6)} %select_n.86, f32[8,8192]{1,0:T(8,128)S(1)} %broadcast_in_dim.49, f32[8,8192]{1,0:T(8,128)S(1)} %fusion.24), kind=kLoop, calls=%fused_computation.28 | loop fusion | flops 786432 | bytes 1572948 | tf_op jit(solution)/shard_map/mul | solution.py:132
  (30 shorter events, 7.7 us)
Async XLA Ops:
  0.0 8.3 %collective-permute-start = (bf16[1,2,32768]{2,1,0:T(2,128)(2,1)}, bf16[1,2,32768]{2,1,0:T(2,128)(2,1)S(1)}, u32[]{:S(2)}, u32[]{:S(2)}) collective-permute-start(bf16[1,2,32768]{2,1,0:T(2,128)(2,1)} %param.3), channel_id=1, source_target_pairs={{0,15},{1,0},{2,1},{3,2},{4,3},{5,4},{6,5},{7,6},{8,7},{9,8},{10,9... | collective-permute-start | bytes 393224 | tf_op jit(solution)/shard_map/ppermute | solution.py:13
  5.4 18.3 %collective-permute-start.3 = (bf16[1,2,32768]{2,1,0:T(2,128)(2,1)}, bf16[1,2,32768]{2,1,0:T(2,128)(2,1)S(1)}, u32[]{:S(2)}, u32[]{:S(2)}) collective-permute-start(bf16[1,2,32768]{2,1,0:T(2,128)(2,1)} %param.3), channel_id=1, source_target_pairs={{0,8},{1,9},{2,10},{3,11},{4,12},{5,13},{6,14},{7,15},{8,0},{9,1},... | collective-permute-start | bytes 393224 | tf_op jit(solution)/shard_map/ppermute | solution.py:13
  9.6 8.0 %collective-permute-start.1 = (bf16[2,2,32768]{2,1,0:T(2,128)(2,1)S(1)}, bf16[2,2,32768]{2,1,0:T(2,128)(2,1)S(1)}, u32[]{:S(2)}, u32[]{:S(2)}) collective-permute-start(bf16[2,2,32768]{2,1,0:T(2,128)(2,1)S(1)} %pad_maximum_fusion.2), channel_id=1, source_target_pairs={{0,14},{1,15},{2,0},{3,1},{4,2},{5,3},{6,4},{7,5},{8,6},{9,7},{10,... | collective-permute-start | bytes 786440 | tf_op jit(solution)/shard_map/ppermute | solution.py:13
  19.2 13.9 %collective-permute-start.2 = (bf16[4,2,32768]{2,1,0:T(2,128)(2,1)S(1)}, bf16[4,2,32768]{2,1,0:T(2,128)(2,1)S(1)}, u32[]{:S(2)}, u32[]{:S(2)}) collective-permute-start(bf16[4,2,32768]{2,1,0:T(2,128)(2,1)S(1)} %pad_maximum_fusion.1), channel_id=1, source_target_pairs={{0,12},{1,13},{2,14},{3,15},{4,0},{5,1},{6,2},{7,3},{8,4},{9,5},{1... | collective-permute-start | bytes 1572872 | tf_op jit(solution)/shard_map/ppermute | solution.py:13
  46.5 3.2 %copy-start = (f32[128,512]{1,0:T(8,128)S(1)}, f32[128,512]{1,0:T(8,128)}, u32[]{:S(2)}) copy-start(f32[128,512]{1,0:T(8,128)} %get-tuple-element.14) | copy-start | bytes 786436
  49.8 2.8 %copy-start.1 = (f32[64,1,512]{2,0,1:T(8,128)S(1)}, f32[64,1,512]{2,0,1:T(8,128)}, u32[]{:S(2)}) copy-start(f32[64,1,512]{2,0,1:T(8,128)} %get-tuple-element.18) | copy-start | bytes 393220
  54.6 16.2 %copy-start.2 = (s32[16]{0:T(128)S(1)}, s32[16]{0:T(128)}, u32[]{:S(2)}) copy-start(s32[16]{0:T(128)} %param.5) | copy-start | bytes 196
  54.6 17.5 %copy-start.3 = (s32[1,16]{1,0:T(1,128)S(1)}, s32[1,16]{1,0:T(1,128)}, u32[]{:S(2)}) copy-start(s32[1,16]{1,0:T(1,128)} %param.4) | copy-start | bytes 196
  65.3 19.7 %all-to-all-start = ((f32[16,1,1,8192]{3,2,1,0:T(1,128)}), f32[16,1,1,8192]{3,2,1,0:T(1,128)S(1)}, u32[]{:S(2)}, u32[]{:S(2)}) async-start(f32[16,1,1,8192]{3,2,1,0:T(1,128)} %constant_dynamic-update-slice_fusion), calls=%async_computation | async-start | bytes 1048576 | tf_op jit(solution)/shard_map/all_to_all | solution.py:129
